TPU v7x, 16 devices: a whole 2x2x2 slice. The times are simulated.
16 devices in a mesh: data: 16 (over z, y, x, core).
Axes of the slice: x: 2, y: 2, z: 2, core: 2. Of those that a mesh axis runs over, the one named last changes fastest.
Arguments:
- x_in: bfloat16 [192, 128, 1024], P('data')
- g_out: bfloat16 [192, 128, 1024], P('data')
- step_emb: bfloat16 [4, 1024], replicated
- w_q: bfloat16 [1024, 16, 64], replicated
- w_k: bfloat16 [1024, 16, 64], replicated
- w_v: bfloat16 [1024, 16, 64], replicated
- w_o: bfloat16 [16, 64, 1024], replicated
- w_up: bfloat16 [1024, 4096], replicated
- w_down: bfloat16 [4096, 1024], replicated
Outputs:
- output 1: float32 [1024, 16, 64], replicated
- output 2: float32 [1024, 16, 64], replicated
- output 3: float32 [1024, 16, 64], replicated
- output 4: float32 [16, 64, 1024], replicated
- output 5: float32 [1024, 4096], replicated
- output 6: float32 [4096, 1024], replicated
- output 7: bfloat16 [192, 128, 1024], P('data')
All inputs are finite; a program needn't handle non-finite values.
Results may differ from a plain program's by a relative error of at most 0.02.
Values are sent between devices in bfloat16 or wider.
A program may use at most 1 GiB of HBM per device.

v0:
```python
import jax
import jax.numpy as jnp
from jax import lax
from jax.sharding import PartitionSpec as P, NamedSharding
import functools

NORM_EPS = 1e-6


def rms_norm(x_val):
    x_f32 = x_val.astype(jnp.float32)
    return (x_f32 * lax.rsqrt(jnp.mean(x_f32 * x_f32, axis=-1, keepdims=True) + NORM_EPS)).astype(jnp.bfloat16)


def gelu_act(z_val):
    return jax.nn.gelu(z_val.astype(jnp.float32), approximate=True).astype(jnp.bfloat16)


def attn_probs(scores, attn_scale):
    return jax.nn.softmax(scores.astype(jnp.float32) * attn_scale, axis=-1).astype(jnp.bfloat16)


def layer_fwd(x_prev, step_vec, weight_set, attn_scale):
    w_qkv, w_o, w_up, w_down = weight_set
    n_heads = w_o.shape[0]
    x_cur = x_prev + step_vec
    u_norm = rms_norm(x_cur)
    qkv_heads = jnp.einsum('bsd,dhe->bshe', u_norm, w_qkv, preferred_element_type=jnp.float32).astype(jnp.bfloat16)
    q_heads = qkv_heads[:, :, :n_heads]
    k_heads = qkv_heads[:, :, n_heads:2 * n_heads]
    v_heads = qkv_heads[:, :, 2 * n_heads:]
    scores = jnp.einsum('bqhe,bkhe->bhqk', q_heads, k_heads, preferred_element_type=jnp.float32).astype(jnp.bfloat16)
    prob_mat = attn_probs(scores, attn_scale)
    mix_heads = jnp.einsum('bhqk,bkhe->bqhe', prob_mat, v_heads, preferred_element_type=jnp.float32).astype(jnp.bfloat16)
    attn_out = jnp.einsum('crif,ife->cre', mix_heads, w_o, preferred_element_type=jnp.float32).astype(jnp.bfloat16)
    h_mid = x_cur + attn_out
    z_up = jnp.dot(rms_norm(h_mid), w_up, preferred_element_type=jnp.float32).astype(jnp.bfloat16)
    y_down = jnp.dot(gelu_act(z_up), w_down, preferred_element_type=jnp.float32).astype(jnp.bfloat16)
    return h_mid + y_down, (x_cur, qkv_heads, mix_heads, h_mid, z_up)


def layer_bwd(d_out, saved_acts, weight_set, attn_scale):
    w_qkv, w_o, w_up, w_down = weight_set
    x_cur, qkv_heads, mix_heads, h_mid, z_up = saved_acts
    n_heads = w_o.shape[0]
    g_act, gelu_pull = jax.vjp(gelu_act, z_up)
    grad_down = jnp.einsum('bsf,bsd->fd', g_act, d_out, preferred_element_type=jnp.float32)
    d_act = jnp.einsum('bsd,fd->bsf', d_out, w_down, preferred_element_type=jnp.float32).astype(jnp.bfloat16)
    (d_up,) = gelu_pull(d_act)
    m_norm, norm_pull_h = jax.vjp(rms_norm, h_mid)
    grad_up = jnp.einsum('bsd,bsf->df', m_norm, d_up, preferred_element_type=jnp.float32)
    d_norm_h = jnp.einsum('bsf,df->bsd', d_up, w_up, preferred_element_type=jnp.float32).astype(jnp.bfloat16)
    (d_mid_norm,) = norm_pull_h(d_norm_h)
    d_mid = d_out + d_mid_norm
    grad_o = jnp.einsum('crif,cre->ife', mix_heads, d_mid, preferred_element_type=jnp.float32)
    d_mix = jnp.einsum('cre,ife->crif', d_mid, w_o, preferred_element_type=jnp.float32).astype(jnp.bfloat16)
    q_heads = qkv_heads[:, :, :n_heads]
    k_heads = qkv_heads[:, :, n_heads:2 * n_heads]
    v_heads = qkv_heads[:, :, 2 * n_heads:]
    scores = jnp.einsum('bqhe,bkhe->bhqk', q_heads, k_heads, preferred_element_type=jnp.float32).astype(jnp.bfloat16)
    prob_mat, prob_pull = jax.vjp(functools.partial(attn_probs, attn_scale=attn_scale), scores)
    d_v = jnp.einsum('bhqk,bqhe->bkhe', prob_mat, d_mix, preferred_element_type=jnp.float32).astype(jnp.bfloat16)
    d_prob = jnp.einsum('bqhe,bkhe->bhqk', d_mix, v_heads, preferred_element_type=jnp.float32).astype(jnp.bfloat16)
    (d_scores,) = prob_pull(d_prob)
    d_q = jnp.einsum('bhqk,bkhe->bqhe', d_scores, k_heads, preferred_element_type=jnp.float32).astype(jnp.bfloat16)
    d_k = jnp.einsum('bhqk,bqhe->bkhe', d_scores, q_heads, preferred_element_type=jnp.float32).astype(jnp.bfloat16)
    d_qkv = jnp.concatenate([d_q, d_k, d_v], axis=2)
    u_norm, norm_pull_x = jax.vjp(rms_norm, x_cur)
    grad_qkv = jnp.einsum('bsd,bshe->dhe', u_norm, d_qkv, preferred_element_type=jnp.float32)
    d_norm_x = jnp.einsum('bshe,dhe->bsd', d_qkv, w_qkv, preferred_element_type=jnp.float32).astype(jnp.bfloat16)
    (d_cur_norm,) = norm_pull_x(d_norm_x)
    return d_mid + d_cur_norm, (grad_qkv, grad_o, grad_up, grad_down)


def micro_pass(x_mb, g_mb, step_emb, weight_set, attn_scale):
    n_layers = step_emb.shape[0]
    x_cur = x_mb
    saved_list = []
    for layer_idx in range(n_layers):
        x_cur, saved_acts = layer_fwd(x_cur, step_emb[layer_idx], weight_set, attn_scale)
        saved_list.append(saved_acts)
    d_cur = g_mb
    grad_sum = tuple(jnp.zeros(w.shape, jnp.float32) for w in weight_set)
    for layer_idx in reversed(range(n_layers)):
        d_cur, layer_grads = layer_bwd(d_cur, saved_list[layer_idx], weight_set, attn_scale)
        grad_sum = tuple(acc_part + new_part for acc_part, new_part in zip(grad_sum, layer_grads))
    return d_cur, grad_sum


def solution(mesh):
    batch_spec = P('data', None, None)

    def per_device(x_loc, g_loc, step_emb, w_q, w_k, w_v, w_o, w_up, w_down):
        n_heads = w_q.shape[1]
        attn_scale = w_q.shape[2] ** -0.5
        weight_set = (jnp.concatenate([w_q, w_k, w_v], axis=1), w_o, w_up, w_down)
        rows_mb = x_loc.shape[0] // 2
        dx_parts = []
        grad_total = tuple(jnp.zeros(w.shape, jnp.float32) for w in weight_set)
        for micro_idx in range(2):
            start_row = micro_idx * rows_mb
            d_x, micro_grads = micro_pass(x_loc[start_row:start_row + rows_mb], g_loc[start_row:start_row + rows_mb], step_emb, weight_set, attn_scale)
            reduced = lax.psum(micro_grads, 'data')
            grad_total = tuple(acc_part + new_part for acc_part, new_part in zip(grad_total, reduced))
            dx_parts.append(d_x)
        grad_qkv, grad_o, grad_up, grad_down = grad_total
        return (grad_qkv[:, :n_heads], grad_qkv[:, n_heads:2 * n_heads], grad_qkv[:, 2 * n_heads:], grad_o, grad_up, grad_down, jnp.concatenate(dx_parts, axis=0))

    return jax.shard_map(per_device, mesh=mesh, in_specs=(batch_spec, batch_spec, P(), P(), P(), P(), P(), P(), P()), out_specs=(P(), P(), P(), P(), P(), P(), batch_spec), check_vma=False)
```

profile of v0, /device:TPU:0, one launch (start us, length us, event | category | flops | bytes accessed | tf_op | source)
XLA Modules:
  0.0 1663.5 jit_solution(16232021598664015229)
XLA Ops:
  83.4 17.4 %fusion.756 = (f32[6,16,128]{2,1,0:T(8,128)S(1)}, f32[6,16,128,128]{2,3,1,0:T(8,128)S(1)}) fusion(bf16[6,16,128,128]{2,3,1,0:T(8,128)(2,1)S(1)} %convolution_convert_fusion.14), kind=kOutput, calls=%fused_computation.900 | output fusion | flops 9437311 | bytes 9486336 | tf_op jit(solution)/shard_map/sub | solution.py:20
  311.1 12.9 fusion.180
  324.0 19.0 %fusion.32 = bf16[6,128,4096]{2,1,0:T(8,128)(2,1)} fusion(bf16[6,128,4096]{2,1,0:T(8,128)(2,1)} %fusion.180, bf16[12,128,1024]{2,1,0:T(8,128)(2,1)S(1)} %copy-done.73, bf16[4096,1024]{1,0:T(8,128)(2,1)} %param.17), kind=kOutput, calls=%fused_computation.92 | convolution fusion | flops 6514802688 | bytes 24117248 | tf_op jit(solution)/shard_map/bsd,fd->bsf/dot_general | solution.py:48
  366.5 18.5 %fusion.20 = bf16[6,128,4096]{2,1,0:T(8,128)(2,1)} fusion(bf16[6,128,4096]{2,1,0:T(8,128)(2,1)} %fusion.168, bf16[12,128,1024]{2,1,0:T(8,128)(2,1)S(1)} %copy-done.73, bf16[4096,1024]{1,0:T(8,128)(2,1)} %param.17), kind=kOutput, calls=%fused_computation.80 | convolution fusion | flops 6514802688 | bytes 24117248 | tf_op jit(solution)/shard_map/bsd,fd->bsf/dot_general | solution.py:48
  480.0 17.7 %fusion.35 = bf16[6,128,4096]{2,1,0:T(8,128)(2,1)S(1)} fusion(bf16[6,128,4096]{2,1,0:T(8,128)(2,1)} %fusion.177, bf16[6,128,1024]{2,1,0:T(8,128)(2,1)S(1)} %fusion.508, bf16[4096,1024]{1,0:T(8,128)(2,1)} %param.17), kind=kOutput, calls=%fused_computation.95 | convolution fusion | flops 6514802688 | bytes 22544384 | tf_op jit(solution)/shard_map/bsd,fd->bsf/dot_general | solution.py:48
  547.2 17.7 %fusion.38 = bf16[6,128,4096]{2,1,0:T(8,128)(2,1)S(1)} fusion(bf16[6,128,4096]{2,1,0:T(8,128)(2,1)} %copy-done.244, bf16[6,128,1024]{2,1,0:T(8,128)(2,1)S(1)} %fusion.506, bf16[4096,1024]{1,0:T(8,128)(2,1)} %param.17), kind=kOutput, calls=%fused_computation.98 | convolution fusion | flops 6514802688 | bytes 22544384 | tf_op jit(solution)/shard_map/bsd,fd->bsf/dot_general | solution.py:48
  616.9 16.7 %fusion.41 = bf16[6,128,4096]{2,1,0:T(8,128)(2,1)S(1)} fusion(bf16[6,128,4096]{2,1,0:T(8,128)(2,1)S(1)} %bitcast.892, bf16[6,128,1024]{2,1,0:T(8,128)(2,1)S(1)} %fusion.504, bf16[4096,1024]{1,0:T(8,128)(2,1)} %param.17), kind=kOutput, calls=%fused_computation.101 | convolution fusion | flops 6514802688 | bytes 22544384 | tf_op jit(solution)/shard_map/bsd,fd->bsf/dot_general | solution.py:48
  664.5 17.9 %fusion.23 = bf16[6,128,4096]{2,1,0:T(8,128)(2,1)S(1)} fusion(bf16[6,128,4096]{2,1,0:T(8,128)(2,1)} %copy-done.243, bf16[6,128,1024]{2,1,0:T(8,128)(2,1)S(1)} %fusion.515, bf16[4096,1024]{1,0:T(8,128)(2,1)} %param.17), kind=kOutput, calls=%fused_computation.83 | convolution fusion | flops 6514802688 | bytes 22544384 | tf_op jit(solution)/shard_map/bsd,fd->bsf/dot_general | solution.py:48
  731.6 17.9 %fusion.26 = bf16[6,128,4096]{2,1,0:T(8,128)(2,1)S(1)} fusion(bf16[6,128,4096]{2,1,0:T(8,128)(2,1)} %copy-done.242, bf16[6,128,1024]{2,1,0:T(8,128)(2,1)S(1)} %fusion.513, bf16[4096,1024]{1,0:T(8,128)(2,1)} %param.17), kind=kOutput, calls=%fused_computation.86 | convolution fusion | flops 6514802688 | bytes 22544384 | tf_op jit(solution)/shard_map/bsd,fd->bsf/dot_general | solution.py:48
  798.6 17.9 %fusion.29 = bf16[6,128,4096]{2,1,0:T(8,128)(2,1)S(1)} fusion(bf16[6,128,4096]{2,1,0:T(8,128)(2,1)} %copy-done.241, bf16[6,128,1024]{2,1,0:T(8,128)(2,1)S(1)} %fusion.511, bf16[4096,1024]{1,0:T(8,128)(2,1)} %param.17), kind=kOutput, calls=%fused_computation.89 | convolution fusion | flops 6514802688 | bytes 22544384 | tf_op jit(solution)/shard_map/bsd,fd->bsf/dot_general | solution.py:48
  859.0 13.5 fusion.655
  926.8 12.9 fusion.751
  939.8 12.8 fusion.748
  952.6 13.0 fusion.745
  965.7 12.8 fusion.740
  978.5 15.3 fusion.737
  993.8 12.7 fusion.209
  1006.5 14.9 fusion.207
  1030.1 13.1 fusion.275
  1043.2 43.8 %fusion.17 = f32[1024,4096]{1,0:T(8,128)} fusion(f32[1024,4096,1]{1,0,2:T(8,128)} %fusion.644, f32[1024,4096,1]{1,0,2:T(8,128)} %fusion.641, f32[1024,4096,1]{1,0,2:T(8,128)} %fusion.638, f32[1024,4096,1]{1,0,2:T(8,128)} %fusion.658, f32[1024,4096,1]{1,0,2:T(8,128)} %fusion.655, f32[1024,4096,1]{1,0,2:T(8,128)} %fusion.652, f32[1024,4096,1]{1,0,2:T(8,128)} %fusion.649, ...), kind=kOutput, calls=%fused_computation.64 | convolution fusion | flops 6474170368 | bytes 142085120 | tf_op jit(solution)/shard_map/bsd,bsf->df/dot_general | solution.py:51
  1087.0 42.9 %fusion.16 = f32[4096,1024]{1,0:T(8,128)} fusion(f32[4096,1024,1]{1,0,2:T(8,128)} %fusion.740, f32[4096,1024,1]{1,0,2:T(8,128)} %fusion.737, f32[4096,1024,1]{1,0,2:T(8,128)} %fusion.207, f32[4096,1024,1]{1,0,2:T(8,128)} %fusion.751, f32[4096,1024,1]{1,0,2:T(8,128)} %fusion.748, f32[4096,1024,1]{1,0,2:T(8,128)} %fusion.745, f32[4096,1024,1]{1,0,2:T(8,128)} %fusion.209, ...), kind=kOutput, calls=%fused_computation.57 | convolution fusion | flops 6503268352 | bytes 142082048 | tf_op jit(solution)/shard_map/bsf,bsd->fd/dot_general | solution.py:47
  1129.9 35.8 %fusion.98 = f32[1024,48,64]{0,2,1:T(8,128)} fusion(f32[1024,48,64,1]{0,2,1,3:T(8,128)} %fusion.398, f32[1024,48,64,1]{0,2,1,3:T(8,128)} %fusion.400, f32[1024,48,64,1]{0,2,1,3:T(8,128)} %fusion.402, f32[1024,48,64,1]{0,2,1,3:T(8,128)} %fusion.404, f32[1024,48,64,1]{0,2,1,3:T(8,128)} %fusion.406, f32[1024,48,64,1]{0,2,1,3:T(8,128)} %fusion.408, ...), kind=kOutput, calls=%fused_computation.159 | convolution fusion | flops 4872732672 | bytes 106959872 | tf_op jit(solution)/shard_map/bsd,bshe->dhe/dot_general | solution.py:69
  1191.3 430.5 %all-reduce.3.cloned.1.call-done = (f32[1024,48,64]{0,2,1:T(8,128)}, f32[16,64,1024]{2,1,0:T(8,128)}, f32[1024,4096]{1,0:T(8,128)}, f32[4096,1024]{1,0:T(8,128)}) async-done(((f32[1024,48,64]{0,2,1:T(8,128)}, f32[16,64,1024]{2,1,0:T(8,128)}, f32[1024,4096]{1,0:T(8,128)}, f32[4096,1024]{1,0:T(8,128)}), (f32[1024,48,64]{0,2,1:T(8,128)}, f32[16,64,1024]{2,1,0:T(8,128)}, f32[1024,4096]{1,0:T(8,128)}, ...) | async-done | bytes 50331664 | tf_op jit(solution)/shard_map/psum | solution.py:103
  1634.1 13.9 copy.181
  (857 shorter events, 783.3 us)
Async XLA Ops:
  7.2 1614.5 %all-reduce.3.cloned.1.call-start = ((), (), s32[]{:S(2)}) async-start(), calls=%async_computation | async-start | bytes 100663296 | tf_op jit(solution)/shard_map/psum | solution.py:103
  8.8 43.6 %copy-start.150 = (bf16[1024]{0:T(1024)(128)(2,1)}, bf16[1024]{0:T(1024)(128)(2,1)S(1)}, u32[]{:S(2)}) copy-start(bf16[1024]{0:T(1024)(128)(2,1)S(1)} %get-tuple-element.13) | copy-start | bytes 6148
  8.8 57.9 %copy-start.201 = (bf16[1024]{0:T(1024)(128)(2,1)}, bf16[1024]{0:T(1024)(128)(2,1)S(1)}, u32[]{:S(2)}) copy-start(bf16[1024]{0:T(1024)(128)(2,1)S(1)} %get-tuple-element.12) | copy-start | bytes 6148
  11.6 24.1 %copy-start.152 = (f32[6,128]{1,0:T(8,128)}, f32[6,128]{1,0:T(8,128)S(1)}, u32[]{:S(2)}) copy-start(f32[6,128]{1,0:T(8,128)S(1)} %fusion.689) | copy-start | bytes 9220
  74.9 29.6 %copy-start.77 = (bf16[6,128,1024]{2,1,0:T(8,128)(2,1)}, bf16[6,128,1024]{2,1,0:T(8,128)(2,1)S(1)}, u32[]{:S(2)}) copy-start(bf16[6,128,1024]{2,1,0:T(8,128)(2,1)S(1)} %get-tuple-element.31) | copy-start | bytes 4718596
  311.1 86.2 %copy-start.37 = (bf16[6,128,1024]{2,1,0:T(8,128)(2,1)}, bf16[6,128,1024]{2,1,0:T(8,128)(2,1)S(1)}, u32[]{:S(2)}) copy-start(bf16[6,128,1024]{2,1,0:T(8,128)(2,1)S(1)} %get-tuple-element.71) | copy-start | bytes 4718596
  311.1 86.2 %copy-start.133 = (f32[6,128]{1,0:T(8,128)}, f32[6,128]{1,0:T(8,128)S(1)}, u32[]{:S(2)}) copy-start(f32[6,128]{1,0:T(8,128)S(1)} %fusion.704) | copy-start | bytes 9220
  401.1 34.6 %copy-start.53 = (bf16[6,128,1024]{2,1,0:T(8,128)(2,1)}, bf16[6,128,1024]{2,1,0:T(8,128)(2,1)S(1)}, u32[]{:S(2)}) copy-start(bf16[6,128,1024]{2,1,0:T(8,128)(2,1)S(1)} %get-tuple-element.24) | copy-start | bytes 4718596
  480.0 29.8 %copy-start.60 = (bf16[6,128,1024]{2,1,0:T(8,128)(2,1)}, bf16[6,128,1024]{2,1,0:T(8,128)(2,1)S(1)}, u32[]{:S(2)}) copy-start(bf16[6,128,1024]{2,1,0:T(8,128)(2,1)S(1)} %fusion.508) | copy-start | bytes 4718596
  547.2 29.6 %copy-start.62 = (bf16[6,128,1024]{2,1,0:T(8,128)(2,1)}, bf16[6,128,1024]{2,1,0:T(8,128)(2,1)S(1)}, u32[]{:S(2)}) copy-start(bf16[6,128,1024]{2,1,0:T(8,128)(2,1)S(1)} %fusion.506) | copy-start | bytes 4718596
  616.9 28.5 %copy-start.8 = (bf16[6,128,1024]{2,1,0:T(8,128)(2,1)}, bf16[6,128,1024]{2,1,0:T(8,128)(2,1)S(1)}, u32[]{:S(2)}) copy-start(bf16[6,128,1024]{2,1,0:T(8,128)(2,1)S(1)} %fusion.504) | copy-start | bytes 4718596
  664.5 29.7 %copy-start.64 = (bf16[6,128,1024]{2,1,0:T(8,128)(2,1)}, bf16[6,128,1024]{2,1,0:T(8,128)(2,1)S(1)}, u32[]{:S(2)}) copy-start(bf16[6,128,1024]{2,1,0:T(8,128)(2,1)S(1)} %fusion.515) | copy-start | bytes 4718596
  731.5 29.7 %copy-start.66 = (bf16[6,128,1024]{2,1,0:T(8,128)(2,1)}, bf16[6,128,1024]{2,1,0:T(8,128)(2,1)S(1)}, u32[]{:S(2)}) copy-start(bf16[6,128,1024]{2,1,0:T(8,128)(2,1)S(1)} %fusion.513) | copy-start | bytes 4718596
  798.6 29.7 %copy-start.68 = (bf16[6,128,1024]{2,1,0:T(8,128)(2,1)}, bf16[6,128,1024]{2,1,0:T(8,128)(2,1)S(1)}, u32[]{:S(2)}) copy-start(bf16[6,128,1024]{2,1,0:T(8,128)(2,1)S(1)} %fusion.511) | copy-start | bytes 4718596
  848.1 24.4 %slice-start.32 = ((s8[6291456]{0:T(1024)(128)(4,1)}), s8[4194304]{0:T(1024)(128)(4,1)S(1)}, s32[]{:S(2)}) async-start(s8[6291456]{0:T(1024)(128)(4,1)} %bitcast.905), calls=%async_computation.33 | async-start | bytes 8388608
  858.9 24.3 %slice-start.30 = ((s8[6291456]{0:T(1024)(128)(4,1)}), s8[4194304]{0:T(1024)(128)(4,1)S(1)}, s32[]{:S(2)}) async-start(s8[6291456]{0:T(1024)(128)(4,1)} %bitcast.903), calls=%async_computation.31 | async-start | bytes 8388608
  926.8 25.8 %slice-start.56 = ((s8[6291456]{0:T(1024)(128)(4,1)}), s8[4194304]{0:T(1024)(128)(4,1)S(1)}, s32[]{:S(2)}) async-start(s8[6291456]{0:T(1024)(128)(4,1)} %bitcast.929), calls=%async_computation.57 | async-start | bytes 8388608
  939.7 25.9 %slice-start.58 = ((s8[6291456]{0:T(1024)(128)(4,1)}), s8[4194304]{0:T(1024)(128)(4,1)S(1)}, s32[]{:S(2)}) async-start(s8[6291456]{0:T(1024)(128)(4,1)} %bitcast.931), calls=%async_computation.59 | async-start | bytes 8388608
  965.6 28.1 %slice-start.60 = ((s8[6291456]{0:T(1024)(128)(4,1)}), s8[4194304]{0:T(1024)(128)(4,1)S(1)}, s32[]{:S(2)}) async-start(s8[6291456]{0:T(1024)(128)(4,1)} %bitcast.933), calls=%async_computation.61 | async-start | bytes 8388608
  1006.5 36.6 %slice-start.22 = ((s8[6291456]{0:T(1024)(128)(4,1)}), s8[4194304]{0:T(1024)(128)(4,1)S(1)}, s32[]{:S(2)}) async-start(s8[6291456]{0:T(1024)(128)(4,1)} %bitcast.895), calls=%async_computation.23 | async-start | bytes 8388608
  1030.1 56.9 %slice-start.20 = ((s8[6291456]{0:T(1024)(128)(4,1)}), s8[4194304]{0:T(1024)(128)(4,1)S(1)}, s32[]{:S(2)}) async-start(s8[6291456]{0:T(1024)(128)(4,1)} %bitcast.893), calls=%async_computation.21 | async-start | bytes 8388608
  1043.2 43.8 %copy-start.9 = (bf16[6,128,1024]{2,1,0:T(8,128)(2,1)S(1)}, bf16[6,128,1024]{2,1,0:T(8,128)(2,1)}, u32[]{:S(2)}) copy-start(bf16[6,128,1024]{2,1,0:T(8,128)(2,1)} %copy-done.8) | copy-start | bytes 4718596
  1043.2 43.8 %slice-start.21 = ((s8[6291456]{0:T(1024)(128)(4,1)}), s8[2097152]{0:T(1024)(128)(4,1)S(1)}, s32[]{:S(2)}) async-start(s8[6291456]{0:T(1024)(128)(4,1)} %bitcast.893), calls=%async_computation.22 | async-start | bytes 4194304
  1087.0 42.9 %copy-start.156 = (f32[6,128]{1,0:T(8,128)S(1)}, f32[6,128]{1,0:T(8,128)}, u32[]{:S(2)}) copy-start(f32[6,128]{1,0:T(8,128)} %copy-done.155) | copy-start | bytes 9220
  (284 other events, 2321.8 us)
Sparse Core Ops, SparseCore 0:
  1165.9 455.7 all-reduce.2
where the time goes:
time: 1670 us; the launch traced here: 1660 us
  matrix products  1040 us (62%)
  waiting for transfers between devices  430 us (26%)
  other arithmetic  115 us (7%)
  local copies, waits for them, and re-layouts  62 us (4%)
  between operations  18.8 us (1%)
    psum x1, waiting for transfers between devices, per_device(): reduced = lax.psum(micro_grads, 'data')  430 us
    dot_general x8, matrix products, layer_bwd(): jnp.einsum('bsd,fd->bsf', d_out, w_down, preferred_element_type=jnp.float32)  143 us
    dot_general x8, matrix products, layer_bwd(): jnp.einsum('bsf,bsd->fd', g_act, d_out, preferred_element_type=jnp.float32)  137 us
    dot_general x8, matrix products, layer_bwd(): jnp.einsum('bsd,bsf->df', m_norm, d_up, preferred_element_type=jnp.float32)  122 us
    dot_general x8, matrix products, layer_bwd(): jnp.einsum('bsd,bshe->dhe', u_norm, d_qkv, preferred_element_type=jnp.flo...  100 us
    dot_general x8, matrix products, layer_bwd(): jnp.einsum('bsf,df->bsd', d_up, w_up, preferred_element_type=jnp.float32)  94 us
    dot_general x8, matrix products, layer_fwd(): jnp.dot(rms_norm(h_mid), w_up, preferred_element_type=jnp.float32)  89.8 us
    dot_general x8, matrix products, layer_bwd(): jnp.einsum('bshe,dhe->bsd', d_qkv, w_qkv, preferred_element_type=jnp.floa...  69.6 us
  transfers between devices with their start and end apart: 1, of which 1 were waited for; matrix products, arithmetic and copies ran while one was open for 2% of the time, Pallas kernels for 0%

commit v1 on v0

v1 whole, which is shorter than its diff:
```python
import functools
import itertools
import math
import jax, jax.numpy as jnp
from jax import lax
from jax.sharding import PartitionSpec as P
from jax.experimental import pallas as pl
from jax.experimental.pallas import tpu as pltpu

BF, F32 = jnp.bfloat16, jnp.float32
EPS = 1e-6
VLIM = 67_043_328
LANE = 128
DEVS, BLOCKS, PARTS, NSUB = 16, 8, 4, 4
SERVE = (((1, 3),), ((3, 6),), ((0, 1), (2, 4)), ())
ABUF = ("sbuf", "dbuf", "pbuf", "gbuf")
C_GELU = math.sqrt(2.0 / math.pi)


def dot(a, b, ca=1, cb=0):
    return lax.dot_general(a, b, (((ca,), (cb,)), ((), ())), preferred_element_type=F32)


def rms(xf):
    r = lax.rsqrt(jnp.mean(xf * xf, axis=-1, keepdims=True) + EPS)
    return (xf * r).astype(BF)


def gelu(z):
    zf = z.astype(F32)
    t = jnp.tanh(C_GELU * (zf + 0.044715 * (zf * zf * zf)))
    return (zf * (0.5 * (1.0 + t))).astype(BF)


def pair_cat(x, lo, hi):
    return jnp.concatenate([x * lo, x * hi], axis=0)


def halves(x):
    return jnp.concatenate([x[:, :LANE], x[:, LANE:]], axis=0)


def qkv_of(ref, item, hw):
    r, c = item
    return (ref[r:r + LANE, i * hw + c:i * hw + c + LANE] for i in range(3))


def pair_groups(R, hw, group):
    items = [(r, c) for r in range(0, R, LANE) for c in range(0, hw, LANE)]
    return [items[i:i + group] for i in range(0, len(items), group)]


def staged(groups, stages):
    n, m = len(groups), len(stages)
    for t in range(n + m - 1):
        for s in reversed(range(m)):
            if 0 <= t - s < n:
                for j, item in enumerate(groups[t - s]):
                    stages[s](item, (t - s) % 2, j)


def softmax_t(st, c2):
    mx = jnp.max(st, axis=0, keepdims=True)
    e = jnp.exp2((st - mx) * c2)
    return e * (1.0 / jnp.sum(e, axis=0, keepdims=True))


def attn_fwd(qkv, mix, R, hw, group, sbuf, pbuf, masks, c2):
    def scores(item, slot, j):
        q, k, _ = qkv_of(qkv, item, hw)
        sbuf[slot, j] = dot(k, pair_cat(q, *masks), 1, 1).astype(BF)

    def probs(item, slot, j):
        pbuf[slot, j] = softmax_t(sbuf[slot, j].astype(F32), c2).astype(BF)

    def mixing(item, slot, j):
        r, c = item
        v = qkv[r:r + LANE, 2 * hw + c:2 * hw + c + LANE]
        mix[r:r + LANE, c:c + LANE] = dot(halves(pbuf[slot, j]), pair_cat(v, *masks), 0, 0).astype(BF)
    staged(pair_groups(R, hw, group), (scores, probs, mixing))


def head_masks():
    lane = lax.broadcasted_iota(jnp.int32, (1, LANE), 1)
    return tuple(m.astype(F32).astype(BF) for m in (lane < LANE // 2, lane >= LANE // 2))


def for_rows(R, chunk, body):
    for r in range(0, R, chunk):
        body(slice(r, r + chunk))


def for_tiles(n, w, body):
    for c in range(0, n, w):
        body(slice(c, c + w))


def qkv_copies(hs, dst, sem, base):
    n = hs[0].shape[0]
    return [pltpu.make_async_copy(h, dst.at[pl.ds(i * n, n)], sem.at[base + i]) for i, h in enumerate(hs)]


def fwd_kernel(cfg, x_hbm, emb_ref, wq_h, wk_h, wv_h, wo_h, wup_h, wdown_h,
               xs_h, us_h, qkv_h, mix_h, hs_h, ms_h, z_h, g_h,
               wqkv, wo, wup, wdown, xin, xs, us, qkv, mix, hs, ms, z, g, sbuf, pbuf, wsem, xsem, osem):
    R, NL, c2, upt, pu = cfg["R"], cfg["L"], cfg["c2"], cfg["upt"], cfg["pu"]
    D, FF, QW = wo.shape[1], wup.shape[1], wo.shape[0]
    b = pl.program_id(0)
    nb = pl.num_programs(0)
    wcopies = qkv_copies((wq_h, wk_h, wv_h), wqkv, wsem, 0) + [pltpu.make_async_copy(h, v, wsem.at[3 + i]) for i, (h, v) in enumerate(((wo_h, wo), (wup_h, wup), (wdown_h, wdown)))]
    row = pl.multiple_of(b * R, R)

    @pl.when(b == 0)
    def _():
        pltpu.make_async_copy(x_hbm.at[pl.ds(0, R)], xin, xsem).start()
        for c in wcopies:
            c.start()

    pltpu.make_async_copy(x_hbm.at[pl.ds(0, R)], xin, xsem).wait()
    masks = head_masks()
    outs = [(xs, xs_h), (us, us_h), (qkv, qkv_h), (mix, mix_h), (hs, hs_h), (ms, ms_h), (z, z_h), (g, g_h)]

    def out_copy(i, l):
        return pltpu.make_async_copy(outs[i][0], outs[i][1].at[l, pl.ds(row, R)], osem.at[i])

    def layer(l, carry):
        notfirst = (b > 0) | (l > 0)
        first = jnp.logical_not(notfirst)

        def free(i):
            @pl.when(notfirst)
            def _():
                out_copy(i, 0).wait()

        def wready(i):
            @pl.when(first)
            def _():
                wcopies[i].wait()

        free(0)
        free(1)
        ch = cfg["ch"]

        def enter(rows):
            xc = xin[rows] + emb_ref[l][0:1]
            xs[rows] = xc
            us[rows] = rms(xc.astype(F32))
        for_rows(R, ch, enter)
        out_copy(0, l).start()
        out_copy(1, l).start()
        for i in range(3):
            wready(i)
        free(2)

        def qkv_tile(cs):
            qkv[:, cs] = dot(us[...], wqkv[cs, :], 1, 1).astype(BF)
        for_tiles(wqkv.shape[0], cfg["nq"], qkv_tile)
        out_copy(2, l).start()
        free(3)
        attn_fwd(qkv, mix, R, QW, cfg["pu"], sbuf, pbuf, masks, c2)
        out_copy(3, l).start()
        wready(3)
        free(4)
        free(5)

        def o_tile(cs):
            hs[:, cs] = xs[:, cs] + dot(mix[...], wo[:, cs]).astype(BF)
        for_tiles(D, cfg["no"], o_tile)
        out_copy(4, l).start()

        def norm_h(rows):
            ms[rows] = rms(hs[rows].astype(F32))
        for_rows(R, ch, norm_h)
        out_copy(5, l).start()
        wready(4)
        free(6)
        free(7)

        def up_tile(cs):
            zz = dot(ms[...], wup[:, cs]).astype(BF)
            z[:, cs] = zz
            g[:, cs] = gelu(zz)
        for_tiles(FF, upt, up_tile)
        out_copy(6, l).start()
        out_copy(7, l).start()
        wready(5)

        @pl.when(l < NL - 1)
        def _():
            def down_tile(cs):
                xin[:, cs] = hs[:, cs] + dot(g[...], wdown[:, cs]).astype(BF)
            for_tiles(D, cfg["nd"], down_tile)
        return carry

    lax.fori_loop(0, NL, layer, 0)

    @pl.when(b + 1 < nb)
    def _():
        pltpu.make_async_copy(x_hbm.at[pl.ds(pl.multiple_of((b + 1) * R, R), R)], xin, xsem).start()

    @pl.when(b + 1 == nb)
    def _():
        for i in range(8):
            out_copy(i, 0).wait()


def fwd(x, emb, wq, wk, wv, wo, wup, wdown, R=512, upt=512, pu=4, nq=1024, no=1024, nd=1024, ch=64, lp=None, **kw):
    T, D = x.shape
    L = emb.shape[0]
    FF, QW = wup.shape[1], wo.shape[0]
    cfg = dict(R=R, L=L, c2=(64 ** -0.5) * math.log2(math.e), upt=upt, pu=pu, nq=nq, no=no, nd=nd, ch=ch, **kw)
    any_ = pl.BlockSpec(memory_space=pl.ANY)
    ws = [D, D, 3 * QW, QW, D, D, FF, FF]
    return pl.pallas_call(
        functools.partial(fwd_kernel, cfg),
        grid=(T // R,),
        out_shape=[jax.ShapeDtypeStruct((L, T, w), BF) for w in ws],
        in_specs=[any_, pl.BlockSpec((L, 16, D), lambda b: (0, 0, 0))] + [any_] * 6,
        out_specs=[any_] * 8,
        scratch_shapes=[pltpu.VMEM((3 * QW, D), BF)] + [pltpu.VMEM(w.shape, BF) for w in (wo, wup, wdown)] + [pltpu.VMEM((R, D), BF)]
        + [pltpu.VMEM((R, w), BF) for w in ws] + [pltpu.VMEM((2, pu, LANE, 2 * LANE), BF)] * 2 + [pltpu.SemaphoreType.DMA((6,)), pltpu.SemaphoreType.DMA, pltpu.SemaphoreType.DMA((8,))],
        compiler_params=pltpu.CompilerParams(vmem_limit_bytes=VLIM, dimension_semantics=("arbitrary",), flags=lp or {}),
        cost_estimate=pl.CostEstimate(flops=2 * L * T * D * (4 * QW + 2 * FF), bytes_accessed=2 * L * T * sum(ws), transcendentals=0),
        name="fwd_layers",
    )(x, jnp.broadcast_to(emb[:, None], (L, 16, D)), wq, wk, wv, wo, wup, wdown)


def rms_vjp(xb, dy):
    xf = xb.astype(F32)
    dyf = dy.astype(F32)
    r = lax.rsqrt(jnp.mean(xf * xf, axis=-1, keepdims=True) + EPS)
    c = jnp.mean(xf * dyf, axis=-1, keepdims=True) * (r * r * r)
    return (r * dyf - xf * c).astype(BF)


def gelu_grad(z, da):
    zf = z.astype(F32)
    z2 = zf * zf
    t = jnp.tanh(zf * (C_GELU + (C_GELU * 0.044715) * z2))
    d = 0.5 * (1.0 + t) + (0.5 * zf) * (1.0 - t * t) * (C_GELU + (3 * 0.044715 * C_GELU) * z2)
    return (da.astype(F32) * d).astype(BF)


def attn_bwd(qkv, dmix, dqkv, R, hw, group, bufs, masks, c2, scale):
    sbuf, dbuf, pbuf, gbuf = bufs

    def at(i, item):
        r, c = item
        return slice(r, r + LANE), slice(i * hw + c, i * hw + c + LANE)

    def scores(item, slot, j):
        q, k, v = qkv_of(qkv, item, hw)
        sbuf[slot, j] = dot(k, pair_cat(q, *masks), 1, 1).astype(BF)
        dbuf[slot, j] = dot(v, pair_cat(dmix[at(0, item)], *masks), 1, 1).astype(BF)

    def probs(item, slot, j):
        p = softmax_t(sbuf[slot, j].astype(F32), c2)
        pdp = p * dbuf[slot, j].astype(F32)
        pbuf[slot, j] = p.astype(BF)
        gbuf[slot, j] = ((pdp - p * jnp.sum(pdp, axis=0, keepdims=True)) * scale).astype(BF)

    def grads(item, slot, j):
        q, k, _ = qkv_of(qkv, item, hw)
        ds = gbuf[slot, j]
        dqkv[at(2, item)] = dot(pbuf[slot, j], pair_cat(dmix[at(0, item)], *masks)).astype(BF)
        dqkv[at(1, item)] = dot(ds, pair_cat(q, *masks)).astype(BF)
        dqkv[at(0, item)] = dot(halves(ds), pair_cat(k, *masks), 0, 0).astype(BF)
    staged(pair_groups(R, hw, group), (scores, probs, grads))


def bwd_kernel(cfg, *refs):
    R, NL, lo, mlp, att = cfg["R"], cfg["NL"], cfg["lo"], cfg["mlp"], cfg["att"]
    names = cfg["names"]
    r = dict(zip(names, refs))
    b = pl.program_id(0)
    nb = pl.num_programs(0)
    row = pl.multiple_of(b * R, R)
    masks = head_masks()
    wn = cfg["weights"]
    wc = {n: [pltpu.make_async_copy(r[n + "_h"], r[n], r["wsem"].at[i])] for i, n in enumerate(wn) if n != "wqkv"}
    if "wqkv" in wn:
        wc["wqkv"] = qkv_copies([r[n + "_h"] for n in ("wq", "wk", "wv")], r["wqkv"], r["wsem"], 4)
    ins = cfg["ins"]
    outs = cfg["outs"]

    def in_copy(n, bb, l):
        rr = pl.ds(pl.multiple_of(bb * R, R), R)
        return pltpu.make_async_copy(r[n + "_h"].at[l, rr], r[n], r["isem"].at[ins.index(n)])

    def out_copy(n, i):
        return pltpu.make_async_copy(r[n], r[n + "_h"].at[i, pl.ds(row, R)], r["osem"].at[outs.index(n)])

    def din_copy(bb):
        return pltpu.make_async_copy(r["din_h"].at[pl.ds(pl.multiple_of(bb * R, R), R)], r["d"], r["dsem"])

    top = lo + NL - 1

    @pl.when(b == 0)
    def _():
        din_copy(0).start()
        for i, n in enumerate(ins):
            in_copy(n, 0, top).start()
            if i < len(wn):
                for c in wc[wn[i]]:
                    c.start()
        for n in wn[len(ins):]:
            for c in wc[n]:
                c.start()

    din_copy(0).wait()

    def layer(i, carry):
        l = top - i
        notfirst = (b > 0) | (i > 0)
        first = jnp.logical_not(notfirst)
        lastl = i == NL - 1
        nb_ = jnp.where(lastl, b + 1, b)
        nl_ = jnp.where(lastl, top, l - 1)

        def free(n):
            @pl.when(notfirst)
            def _():
                out_copy(n, 0).wait()

        def wready(n):
            @pl.when(first)
            def _():
                for c in wc[n]:
                    c.wait()

        def ready(n):
            in_copy(n, 0, 0).wait()

        def prefetch(n):
            @pl.when(nb_ < nb)
            def _():
                in_copy(n, nb_, nl_).start()

        d, tmp = r["d"], r["tmp"]
        if mlp:
            z, hs, dup, wdown, wup = r["z"], r["hs"], r["dup"], r["wdown"], r["wup"]
            if att:
                free("dout")
                r["dout"][...] = d[...]
                out_copy("dout", NL - 1 - i).start()
            ready("z")
            wready("wdown")
            free("dup")
            ft = cfg["ft"]

            def act_tile(cs):
                da = dot(d[...], wdown[cs, :], 1, 1).astype(BF)
                dup[:, cs] = gelu_grad(z[:, cs], da)
            for_tiles(dup.shape[1], ft, act_tile)
            out_copy("dup", NL - 1 - i).start()
            prefetch("z")
            wready("wup")


            def nh_tile(cs):
                tmp[:, cs] = dot(dup[...], wup[cs, :], 1, 1).astype(BF)
            for_tiles(tmp.shape[1], cfg["nt"], nh_tile)
            ready("hs")
            free("dmid")

            def mid_rows(rows):
                r["dmid"][rows] = d[rows] + rms_vjp(hs[rows], tmp[rows])
            for_rows(R, cfg["ch"], mid_rows)
            prefetch("hs")
            out_copy("dmid", NL - 1 - i).start()
        if att:
            dm = r["dmid"] if mlp else d
            qkv, xs, dqkv, wo, wqkv = r["qkv"], r["xs"], r["dqkv"], r["wo"], r["wqkv"]
            wready("wo")


            def mix_tile(cs):
                tmp[:, cs] = dot(dm[...], wo[cs, :], 1, 1).astype(BF)
            for_tiles(tmp.shape[1], cfg["nt"], mix_tile)
            ready("qkv")
            free("dqkv")
            hw = wo.shape[0]

            attn_bwd(qkv, tmp, dqkv, R, hw, cfg["pu"], [r[n] for n in ABUF], masks, cfg["c2"], cfg["scale"])
            prefetch("qkv")
            out_copy("dqkv", NL - 1 - i).start()
            wready("wqkv")


            def nx_tile(cs):
                tmp[:, cs] = dot(dqkv[...], wqkv[:, cs]).astype(BF)
            for_tiles(tmp.shape[1], cfg["nt"], nx_tile)
            ready("xs")

            def out_rows(rows):
                d[rows] = dm[rows] + rms_vjp(xs[rows], tmp[rows])
            for_rows(R, cfg["ch"], out_rows)
            prefetch("xs")
        return carry

    lax.fori_loop(0, NL, layer, 0)
    if att:
        dfin = pltpu.make_async_copy(r["d"], r["dfin_h"].at[pl.ds(row, R)], r["fsem"])
        dfin.start()
        dfin.wait()

    @pl.when(b + 1 < nb)
    def _():
        din_copy(b + 1).start()

    @pl.when(b + 1 == nb)
    def _():
        for n in outs:
            out_copy(n, 0).wait()


def bwd(din, saved, weights, NL, lo, mlp=True, att=True, R=512, ft=512, pu=4, ch=64, nt=1024, lp=None, **kw):
    T, D = din.shape
    FF = weights["wup"].shape[1] if mlp else 0
    wn = (["wdown", "wup"] if mlp else []) + (["wo", "wqkv"] if att else [])
    wn_h = [m for n in wn for m in (("wq", "wk", "wv") if n == "wqkv" else (n,))]
    ins = (["z", "hs"] if mlp else []) + (["qkv", "xs"] if att else [])
    outs = (["dout"] if mlp and att else []) + (["dup", "dmid"] if mlp else []) + (["dqkv"] if att else [])
    ow = dict(dout=D, dup=FF, dmid=D, dqkv=saved["qkv"].shape[2] if att else 0)
    out_shape = [jax.ShapeDtypeStruct((NL, T, ow[n]), BF) for n in outs] + ([jax.ShapeDtypeStruct((T, D), BF)] if att else [])
    names = ["din_h"] + [n + "_h" for n in ins] + [n + "_h" for n in wn_h] + [n + "_h" for n in outs] + (["dfin_h"] if att else [])
    scratch = [("d", (R, D)), ("tmp", (R, D))] + [(n, (R, saved[n].shape[2])) for n in ins] + [(n, (3 * weights["wq"].shape[0], D) if n == "wqkv" else weights[n].shape) for n in wn] + [(n, (R, ow[n])) for n in outs] + [(n, (2, pu, LANE, 2 * LANE)) for n in ABUF if att]
    names += [n for n, _ in scratch] + ["wsem", "isem", "osem", "dsem", "fsem"]
    cfg = dict(R=R, NL=NL, lo=lo, mlp=mlp, att=att, ft=ft, pu=pu, ch=ch, nt=nt, names=names, weights=wn, ins=ins, outs=outs,
               c2=(64 ** -0.5) * math.log2(math.e), scale=64 ** -0.5, **kw)
    any_ = pl.BlockSpec(memory_space=pl.ANY)
    res = pl.pallas_call(
        functools.partial(bwd_kernel, cfg),
        grid=(T // R,),
        out_shape=out_shape,
        in_specs=[any_] * (1 + len(ins) + len(wn_h)),
        out_specs=[any_] * len(out_shape),
        scratch_shapes=[pltpu.VMEM(s, BF) for _, s in scratch] + [pltpu.SemaphoreType.DMA((8,))] + [pltpu.SemaphoreType.DMA((4,))] * 2 + [pltpu.SemaphoreType.DMA] * 2,
        compiler_params=pltpu.CompilerParams(vmem_limit_bytes=VLIM, dimension_semantics=("arbitrary",), flags=lp or {}),
        cost_estimate=pl.CostEstimate(flops=2 * NL * T * D * (2 * FF * mlp + 4 * D * att), bytes_accessed=2 * NL * T * (2 * FF * mlp + 8 * D), transcendentals=0),
        name="bwd_%d_%d%s%s" % (lo, NL, "m" if mlp else "", "a" if att else ""),
    )(din, *[saved[n] for n in ins], *[weights[n] for n in wn_h])
    return dict(zip(outs + (["dfin"] if att else []), res))


def wgrad_kernel(cfg, *refs):
    segs, RB, CU, lhs_res, sw = (cfg[k] for k in ("segs", "RB", "CU", "lhs_res", "sw"))
    ends = list(itertools.accumulate(n for _, _, n in segs))
    NU, P, rb2 = ends[-1], PARTS, 2 * RB
    res_h, str_h, pos = [], [], 0
    for na, nb, _ in segs:
        pair = refs[pos:pos + na], refs[pos + na:pos + na + nb]
        pos += na + nb
        res_h.append(pair[not lhs_res])
        str_h.append(pair[lhs_res])
    out, res, strip, acc, *rv = refs[pos:pos + 8]
    rsem, tsem, csem, ssem, qsem = refs[pos + 8:]
    cp = CU // P
    mb = min(2 * LANE, res.shape[1])
    rc = mb if lhs_res else 2 * mb
    nsub = NSUB
    me = lax.axis_index("data")
    bc = me % 2
    bits = [(me // 2 ** (d + 1)) % 2 for d in range(3)]
    core = me + 1 - 2 * bc

    def pick(be, vals):
        return jnp.where(be == 0, vals[0], jnp.where(be == 1, vals[1], vals[2]))

    def nbr(be):
        return me + pick(be, [(1 - 2 * bits[d]) * 2 ** (d + 1) for d in range(3)])

    def pieces(hs, dst, sem, cols):
        slabs = [h.at[q, :, cols] for h in hs for q in range(h.shape[0])]
        n = dst.shape[0] // len(slabs)
        return [pltpu.make_async_copy(h, dst.at[pl.ds(i * n, n)], sem) for i, h in enumerate(slabs)]

    def res_copies(k, j):
        return pieces(res_h[k], res.at[:, pl.ds(j * rc, rc)], rsem.at[j], pl.ds(j * rc, rc))

    def strip_copies(k, u):
        return pieces(str_h[k], strip.at[u % 2], tsem.at[u % 2], pl.ds(pl.multiple_of((u - (ends[k] - segs[k][2])) * sw, sw), sw))

    def start(cs):
        for c in cs:
            c.start()

    def wait(cs):
        for c in cs:
            c.wait()

    def start_strip(u):
        for k, e in enumerate(ends):
            pl.when((u >= e - segs[k][2]) & (u < e))(lambda: start(strip_copies(k, u)))

    start(strip_copies(0, 0))
    for j in range(res.shape[1] // rc):
        start(res_copies(0, j))
    bar = pltpu.get_barrier_semaphore()
    peers = [core] + [nbr(d) for d in range(3)]
    for t in peers:
        pl.semaphore_signal(bar, inc=1, device_id=(t,), device_id_type=pl.DeviceIdType.MESH)
    pl.semaphore_wait(bar, len(peers))

    def rcopy(src, dst, ss, rs, dev):
        return pltpu.make_async_remote_copy(src_ref=src, dst_ref=dst, send_sem=ss, recv_sem=rs, device_id=(dev,), device_id_type=pl.DeviceIdType.MESH)

    def core_copy(v, p):
        return rcopy(acc.at[v % 2, :, 1 - bc, :, pl.ds(p * cp, cp)], rv[0].at[v, p], csem.at[v % 2, p], qsem.at[0, v, p], core)

    def stage_copy(s, v, p):
        return rcopy(rv[0].at[v, p, pl.ds(0, BLOCKS >> s)], rv[s].at[v, p], ssem.at[s - 1, v, p], qsem.at[s, v, p], core)

    def stage(s, v):
        for p in range(P):
            order = [(v + p + d) % 3 for d in range(3)]
            wt = [pick(be, [2 ** d for d in range(3)]) for be in order]
            mine = [pick(be, bits) for be in order]
            held = [sum([mine[d] * wt[d] for d in range(s - (s > 0))], 0)]

            def blocks(lead, d0):
                for f in itertools.product(range(2), repeat=3 - d0):
                    yield lead + sum([b * w for b, w in zip(f, wt[d0:])], 0)
            cols = slice(p * cp, (p + 1) * cp)
            if s == 0:
                core_copy(v, p).wait_recv()
                for k in range(BLOCKS):
                    rv[0][v, p, k] += acc[v % 2, k, bc, :, cols]
            else:
                stage_copy(s, v, p).wait_recv()
                keep = held[0] + mine[s - 1] * wt[s - 1]
                for m, k in enumerate(blocks(keep, s)):
                    total = rv[0][v, p, k] + rv[s][v, p, m]
                    if s < 3:
                        rv[0][v, p, k] = total
                    elif lhs_res:
                        out[:, pl.ds(pl.multiple_of(v * CU + p * cp, LANE), cp)] = total
                    else:
                        out[v, :, cols] = total
                held[0] = keep
            if s < 3:
                for m, k in enumerate(blocks(held[0] + (1 - mine[s]) * wt[s], s + 1)):
                    rcopy(rv[0].at[v, p, k], rv[s + 1].at[v, p, m], ssem.at[s, v, p], qsem.at[s + 1, v, p], nbr(order[s])).start()

    def serve(s, v):
        pl.when((v >= 0) & (v < NU))(lambda: stage(s, v))

    def sub(u, i):
        mi, ni = (i, 0) if lhs_res else (i % 2, i // 2)
        j = mi if lhs_res else ni
        if lhs_res or mi == 0:
            for k, e in enumerate(ends):
                pl.when(u == e - segs[k][2])(lambda: wait(res_copies(k, j)))
        ms, ns, kk = slice(mi * mb, (mi + 1) * mb), slice(ni * sw, (ni + 1) * sw), mb // rb2
        lhs, rhs = (res[:, ms], strip[u % 2]) if lhs_res else (strip[u % 2, :, ms], res[:, ns])
        acc[u % 2, mi * kk:(mi + 1) * kk, :, :, ns] = dot(lhs, rhs, 0, 0).reshape(kk, 2, RB, sw)
        if i == 0:
            start_strip(u + 1)
        for k, e in enumerate(ends[:-1]):
            pl.when(u == e - 1)(lambda: start(res_copies(k + 1, j)))

    def unit(u, carry):
        live = u < NU

        @pl.when(live)
        def _():
            wait(pieces(str_h[0], strip.at[u % 2], tsem.at[u % 2], pl.ds(0, sw)))
            pl.when(u > 1)(lambda: [core_copy(u, p).wait_send() for p in range(P)] and None)
        for i in range(nsub):
            pl.when(live)(lambda: sub(u, i))
            for s, lag in SERVE[i]:
                serve(s, u - lag)
        pl.when(live)(lambda: [core_copy(u, p).start() for p in range(P)] and None)
        return carry
    lax.fori_loop(0, NU + SERVE[1][0][1], unit, 0)

    for v in range(max(0, NU - 2), NU):
        for p in range(P):
            core_copy(v, p).wait_send()

    def drain(v, carry):
        for p in range(P):
            for s in range(1, len(rv)):
                stage_copy(s, v, p).wait_send()
        return carry
    lax.fori_loop(0, NU, drain, 0)


def wgrad(segments, lhs_res, cid, name, sw=512):
    (a0, b0), K = segments[0], sum(a.shape[0] * a.shape[1] for a in segments[0][0])
    WA, WB = a0[0].shape[2], b0[0].shape[2]
    segs = [(len(a), len(b), (b if lhs_res else a)[0].shape[2] // sw) for a, b in segments]
    NU = sum(n for _, _, n in segs)
    WR, RU, CU = (WA, WA, sw) if lhs_res else (WB, sw, WB)
    RB, cp = RU // DEVS, CU // PARTS
    out_sd = jax.ShapeDtypeStruct((RB, NU * sw) if lhs_res else (NU, RB, CU), F32)
    any_ = pl.BlockSpec(memory_space=pl.ANY)
    dma = pltpu.SemaphoreType.DMA
    ops = [x for a, b in segments for x in (*a, *b)]
    return pl.pallas_call(
        functools.partial(wgrad_kernel, dict(segs=segs, RB=RB, CU=CU, lhs_res=lhs_res, sw=sw)),
        out_shape=out_sd,
        in_specs=[any_] * len(ops),
        out_specs=pl.BlockSpec(memory_space=pltpu.VMEM),
        scratch_shapes=[pltpu.VMEM((K, WR), BF), pltpu.VMEM((2, K, sw), BF), pltpu.VMEM((2, BLOCKS, 2, RB, CU), F32)]
        + [pltpu.VMEM((NU, PARTS, BLOCKS >> s, RB, cp), F32) for s in range(NSUB)]
        + [dma((NSUB,)), dma((2,)), dma((2, PARTS)), dma((NSUB - 1, NU, PARTS)), dma((NSUB, NU, PARTS))],
        compiler_params=pltpu.CompilerParams(vmem_limit_bytes=VLIM, collective_id=cid, has_side_effects=True),
        cost_estimate=pl.CostEstimate(flops=2 * K * RU * CU * NU, bytes_accessed=2 * K * (WA + WB), transcendentals=0),
        name=name,
    )(*ops)


def copy_kernel(plan, *refs):
    n = len(plan)
    srcs, dsts, (buf, isem, osem) = refs[:n], refs[n:2 * n], refs[2 * n:]
    depth, rows, width = buf.shape
    jobs = []
    for (r0, c0), src, dst in zip(plan, srcs, dsts):
        for c in range(0, dst.shape[1], width):
            jobs += [(src.at[pl.ds(r0 + r, rows), pl.ds(c0 + c, width)], dst.at[pl.ds(r, rows), pl.ds(c, width)]) for r in range(0, dst.shape[0], rows)]

    def cin(i):
        return pltpu.make_async_copy(jobs[i][0], buf.at[i % depth], isem.at[i % depth])

    def cout(i):
        return pltpu.make_async_copy(buf.at[i % depth], jobs[i][1], osem.at[i % depth])
    ahead = depth // 2
    for i in range(min(ahead, len(jobs))):
        cin(i).start()
    for i in range(len(jobs)):
        j = i + ahead
        if j < len(jobs):
            if j >= depth:
                cout(j - depth).wait()
            cin(j).start()
        cin(i).wait()
        cout(i).start()
    for i in range(max(0, len(jobs) - depth), len(jobs)):
        cout(i).wait()


def copy_out(parts, n_rows=None, rows=512, depth=16):
    any_ = pl.BlockSpec(memory_space=pl.ANY)
    outs = [jax.ShapeDtypeStruct((n_rows or a.shape[0], w), F32) for a, _, _, w in parts]
    dma = pltpu.SemaphoreType.DMA((depth,))
    size = sum(o.size for o in outs)
    return pl.pallas_call(
        functools.partial(copy_kernel, [(r, c) for _, r, c, _ in parts]),
        out_shape=outs,
        in_specs=[any_] * len(parts),
        out_specs=[any_] * len(parts),
        scratch_shapes=[pltpu.VMEM((depth, rows, min(o.shape[1] for o in outs)), F32), dma, dma],
        compiler_params=pltpu.CompilerParams(vmem_limit_bytes=VLIM),
        cost_estimate=pl.CostEstimate(flops=size * rows, bytes_accessed=2 * size, transcendentals=0),
        name="copy_out",
    )(*[a for a, _, _, _ in parts])


def solution(mesh):
    batch_spec = P('data', None, None)

    def per_device(x_loc, g_loc, step_emb, w_q, w_k, w_v, w_o, w_up, w_down):
        n_seq, seq, d = x_loc.shape
        heads, hd = w_q.shape[1], w_q.shape[2]
        qw = heads * hd
        t = n_seq * seq
        flat_t = [w.transpose(1, 2, 0).reshape(qw, d) for w in (w_q, w_k, w_v)]
        weights = dict(wq=flat_t[0], wk=flat_t[1], wv=flat_t[2], wo=w_o.reshape(qw, d), wup=w_up, wdown=w_down)
        n_layers = step_emb.shape[0]
        xs, us, qkv, mix, hs, ms, z, g = fwd(x_loc.reshape(t, d), step_emb, *flat_t, weights["wo"], w_up, w_down)
        saved = dict(xs=xs, qkv=qkv, hs=hs, z=z)
        top = bwd(g_loc.reshape(t, d), saved, weights, n_layers - 1, 1)
        d0 = top["dfin"]
        down = wgrad([([g], [d0[None], top["dout"]])], False, 1, "wgrad_down")
        d0, down = lax.optimization_barrier((d0, down))
        ag_down = lax.all_gather(down, 'data', axis=1, tiled=True)
        low = bwd(d0, saved, weights, 1, 0, att=False)
        dmid0 = low["dmid"]
        upo = wgrad([([ms], [low["dup"], top["dup"]]), ([mix], [dmid0, top["dmid"]])], True, 2, "wgrad_up_o")
        dmid0, upo, ag_down = lax.optimization_barrier((dmid0, upo, ag_down))
        ag_upo = lax.all_gather(upo, 'data', axis=0, tiled=True)
        bot = bwd(dmid0[0], saved, weights, 1, 0, mlp=False)
        gqkv = wgrad([([bot["dqkv"], top["dqkv"]], [us])], False, 3, "wgrad_qkv")
        gqkv, ag_upo = lax.optimization_barrier((gqkv, ag_upo))
        ag_qkv = lax.all_gather(gqkv, 'data', axis=1, tiled=True)
        ff = w_up.shape[1]
        gup, go, gdown = copy_out([(ag_upo, 0, 0, ff), (ag_upo, 0, ff, d), (ag_down.reshape(w_down.shape), 0, 0, d)])
        flat = ag_qkv.reshape(3 * qw, d)
        gq, gk, gv = (w.reshape(heads, hd, d).transpose(2, 0, 1) for w in copy_out([(flat, i * qw, 0, d) for i in range(3)], qw))
        return (gq, gk, gv, go.reshape(heads, hd, d), gup, gdown, bot["dfin"].reshape(x_loc.shape))

    return jax.shard_map(per_device, mesh=mesh, in_specs=(batch_spec, batch_spec, P(), P(), P(), P(), P(), P(), P()), out_specs=(P(), P(), P(), P(), P(), P(), batch_spec), check_vma=False)
```

time: 1670 us -> 950 us (0.57)
  matrix products: 1040 us -> 0 us
  Pallas kernels: 0 us -> 894 us
  waiting for transfers between devices: 430 us -> 36.2 us
  other arithmetic: 115 us -> 0 us
  local copies, waits for them, and re-layouts: 62 us -> 1.36 us
    dot_general x142 -> x0, matrix products: 1040 us -> none  [the longest x8 143 us: layer_bwd(): jnp.einsum('bsd,fd->bsf', d_out, w_down, preferred_element_type=jnp.float32)]
    pallas_call x0 -> x9, Pallas kernels: none -> 894 us  [the longest x3 339 us: bwd(): pl.pallas_call(functools.partial(bwd_kernel, cfg), grid=(T // R,), out_sh...]
    psum x1 -> x0, waiting for transfers between devices: 430 us -> none  [per_device(): reduced = lax.psum(micro_grads, 'data')]
    sub x8 -> x0, other arithmetic: 60.5 us -> none  [attn_probs(): jax.nn.softmax(scores.astype(jnp.float32) * attn_scale, axis=-1)]
    unnamed x617 -> x0, local copies, waits for them, and re-layouts: 50.2 us -> none
    all_gather x0 -> x3, waiting for transfers between devices: none -> 36.2 us  [the longest x1 36.1 us: per_device(): ag_qkv = lax.all_gather(gqkv, 'data', axis=1, tiled=True)]
    convert_element_type x16 -> x0, other arithmetic: 24.2 us -> none  [the longest x8 15.6 us: attn_probs(): scores.astype(jnp.float32) * attn_scale]
    add x14 -> x0, other arithmetic: 18.2 us -> none  [the longest x7 9.4 us: layer_bwd(): d_mid = d_out + d_mid_norm]
  transfers between devices with their start and end apart: 1 -> 3, of which waited for: 1 -> 1; matrix products, arithmetic and copies ran while one was open for 2% -> 0% of each run, Pallas kernels for 0% -> 33%
where the time goes in v1:
time: 950 us; the launch traced here: 946 us
  Pallas kernels  894 us (94%)
  waiting for transfers between devices  36.2 us (4%)
  between operations  14.3 us (2%)
    pallas_call x3, Pallas kernels, bwd(): pl.pallas_call(functools.partial(bwd_kernel, cfg), grid=(T // R,), out_sh...  339 us
    pallas_call x3, Pallas kernels, wgrad(): pl.pallas_call(functools.partial(wgrad_kernel, dict(segs=segs, RB=RB, CU=...  289 us
    pallas_call x1, Pallas kernels, fwd(): pl.pallas_call(functools.partial(fwd_kernel, cfg), grid=(T // R,), out_sh...  231 us
    all_gather x1, waiting for transfers between devices, per_device(): ag_qkv = lax.all_gather(gqkv, 'data', axis=1, tiled=True)  36.1 us
    pallas_call x2, Pallas kernels, copy_out(): pl.pallas_call(functools.partial(copy_kernel, [(r, c) for _, r, c, _ in p...  35.1 us
  transfers between devices with their start and end apart: 3, of which 1 were waited for; matrix products, arithmetic and copies ran while one was open for 0% of the time, Pallas kernels for 33%

profile of v1, /device:TPU:0, one launch (start us, length us, event | category | flops | bytes accessed | tf_op | source)
XLA Modules:
  0.0 945.8 jit_solution(15845098972629824908)
XLA Ops:
  7.2 0.0 all-gather.4.cloned.1.call-start
  7.2 1.4 broadcast_in_dim.4.emb_ref
  8.6 231.1 %fwd_layers.1 = (bf16[4,1536,1024]{2,1,0:T(8,128)(2,1)}, bf16[4,1536,1024]{2,1,0:T(8,128)(2,1)}, bf16[4,1536,3072]{2,1,0:T(8,128)(2,1)}, bf16[4,1536,1024]{2,1,0...) custom-call(bf16[1536,1024]{1,0:T(8,128)(2,1)} %bitcast.48, ...), custom_call_target="tpu_custom_call" | custom-call | flops 154618822656 | bytes 201326592 | tf_op jit(solution)/shard_map/fwd_layers/pallas_call | solution.py:214
  239.7 246.9 %bwd_1_3ma.1 = (bf16[3,1536,1024]{2,1,0:T(8,128)(2,1)}, bf16[3,1536,4096]{2,1,0:T(8,128)(2,1)}, bf16[3,1536,1024]{2,1,0:T(8,128)(2,1)}, bf16[3,1536,3072]{2,1,0:T(8,128)(2,1)}, bf16[1536,1024]{1,0:T(8,128)(2,1)}) custom-call(bf16[1536,1024]{1,0:T(8,128)(2,1)} %bitcast.49, bf16[4,1536,4096]{2,1,0:T(8,128)(2,1)} %get-tuple-element.37.refs_1_, ...), custom_call_target="tpu_custom_call" | custom-call | flops 115964116992 | bytes 150994944 | tf_op jit(solution)/shard_map/bwd_1_3ma/pallas_call | solution.py:432
  486.6 93.0 %wgrad_down.1 = f32[8,32,1024]{2,1,0:T(8,128)} custom-call(bf16[4,1536,4096]{2,1,0:T(8,128)(2,1)} %get-tuple-element.42.refs_0_, bf16[1,1536,1024]{2,1,0:T(8,128)(2,1)} %bitcast.51, bf16[3,1536,1024]{2,1,0:T(8,128)(2,1)} %get-tuple-element.43.refs_2_), custom_call_target="tpu_custom_call" | custom-call | flops 51539607552 | bytes 62914560 | tf_op jit(solution)/shard_map/wgrad_down/pallas_call | solution.py:600
  579.6 0.0 all-gather.4.cloned.1.call-update
  579.7 0.0 all-gather.6.cloned.1.call-start
  579.7 50.1 %bwd_0_1m.1 = (bf16[1,1536,4096]{2,1,0:T(8,128)(2,1)}, bf16[1,1536,1024]{2,1,0:T(8,128)(2,1)}) custom-call(bf16[1536,1024]{1,0:T(8,128)(2,1)} %get-tuple-element.44.refs_0_, bf16[4,1536,4096]{2,1,0:T(8,128)(2,1)} %get-tuple-element.37.refs_1_, bf16[4,1536,1024]{2,1,0:T(8,128)(2,1)} %get-tuple-element.38.refs_2_, bf16[4096,1024]{1,0:T(8,128)(2,1)} %refs_3_.1, ...), custom_call_target="tpu_custom_call" | custom-call | flops 25769803776 | bytes 50331648 | tf_op jit(solution)/shard_map/bwd_0_1m/pallas_call | solution.py:432
  629.8 106.3 %wgrad_up_o.1 = f32[64,5120]{1,0:T(8,128)} custom-call(bf16[4,1536,1024]{2,1,0:T(8,128)(2,1)} %get-tuple-element.46.refs_0_, bf16[1,1536,4096]{2,1,0:T(8,128)(2,1)} %get-tuple-element.47.refs_1_, bf16[3,1536,4096]{2,1,0:T(8,128)(2,1)} %get-tuple-element.48.refs_2_, bf16[4,1536,1024]{2,1,0:T(8,128)(2,1)} %get-tuple-element.49.refs_3_, ...), custom_call_target="tpu_custom_call" | custom-call | flops 64424509440 | bytes 62914560 | tf_op jit(solution)/shard_map/wgrad_up_o/pallas_call | solution.py:600
  736.1 0.0 all-gather.4.cloned.1.call-done
  736.1 0.0 all-gather.6.cloned.1.call-update
  736.2 0.0 all-gather.8.cloned.1.call-start
  736.2 41.5 %bwd_0_1a.1 = (bf16[1,1536,3072]{2,1,0:T(8,128)(2,1)}, bf16[1536,1024]{1,0:T(8,128)(2,1)}) custom-call(bf16[1536,1024]{1,0:T(8,128)(2,1)} %bitcast.31, bf16[4,1536,3072]{2,1,0:T(8,128)(2,1)} %get-tuple-element.39.refs_3_.refs_1_, bf16[4,1536,1024]{2,1,0:T(8,128)(2,1)} %get-tuple-element.40.refs_4_.refs_2_, bf16[1024,1024]{1,0:T(8,128)(2,1)} %bitcast.43, ...), custom_call_target="tpu_custom_call" | custom-call | flops 12884901888 | bytes 25165824 | tf_op jit(solution)/shard_map/bwd_0_1a/pallas_call | solution.py:432
  777.8 89.7 %wgrad_qkv.1 = f32[6,32,1024]{2,1,0:T(8,128)} custom-call(bf16[1,1536,3072]{2,1,0:T(8,128)(2,1)} %get-tuple-element.53.refs_0_, bf16[3,1536,3072]{2,1,0:T(8,128)(2,1)} %get-tuple-element.54.refs_1_, bf16[4,1536,1024]{2,1,0:T(8,128)(2,1)} %get-tuple-element.55.refs_2_), custom_call_target="tpu_custom_call" | custom-call | flops 38654705664 | bytes 50331648 | tf_op jit(solution)/shard_map/wgrad_qkv/pallas_call | solution.py:600
  867.5 0.0 all-gather.6.cloned.1.call-done.refs_0_.refs_1_
  867.5 0.0 all-gather.8.cloned.1.call-update
  867.5 25.9 %copy_out.3 = (f32[1024,4096]{1,0:T(8,128)}, f32[1024,1024]{1,0:T(8,128)}, f32[4096,1024]{1,0:T(8,128)}) custom-call(f32[1024,5120]{1,0:T(8,128)} %all-gather.6.cloned.1.call-done.refs_0_.refs_1_, f32[1024,5120]{1,0:T(8,128)} %all-gather.6.cloned.1.call-done.refs_0_.refs_1_, f32[4096,1024]{1,0:T(8,128)} %bitcast.30), custom_call_target="tpu_custom_call" | custom-call | flops 4831838208 | bytes 18874368 | tf_op jit(solution)/shard_map/copy_out/pallas_call | solution.py:648
  893.4 36.1 %all-gather.8.cloned.1.call-done = f32[6,512,1024]{2,1,0:T(8,128)} async-done(((f32[6,32,1024]{2,1,0:T(8,128)}), f32[6,512,1024]{2,1,0:T(8,128)}) %all-gather.8.cloned.1.call-update) | async-done | bytes 12582928 | tf_op jit(solution)/shard_map/all_gather | solution.py:686
  929.6 9.2 copy_out.2
Async XLA Ops:
  7.2 729.0 %all-gather.4.cloned.1.call-start = ((), (), s32[]{:S(2)}) async-start(), calls=%async_computation | async-start | bytes 17825792 | tf_op jit(solution)/shard_map/all_gather | solution.py:677
  579.7 287.8 %all-gather.6.cloned.1.call-start = ((), (), s32[]{:S(2)}) async-start(), calls=%async_computation.1 | async-start | bytes 22282240 | tf_op jit(solution)/shard_map/all_gather | solution.py:682
  736.2 193.4 %all-gather.8.cloned.1.call-start = ((), (), s32[]{:S(2)}) async-start(), calls=%async_computation.2 | async-start | bytes 13369344 | tf_op jit(solution)/shard_map/all_gather | solution.py:686
Sparse Core Ops, SparseCore 0:
  579.8 79.6 all-gather.3
  736.3 114.3 all-gather.5
  867.7 61.8 all-gather.7
